TPU v7x, 32 devices: a whole 2x2x4 slice. The times are simulated.
32 devices in a mesh: gx: 8 (over y, x, core), gy: 4 (over z).
Axes of the slice: x: 2, y: 2, z: 4, core: 2. Of those that a mesh axis runs over, the one named last changes fastest.
Arguments:
- right_side: float32 [3, 128, 32, 256], P(None, 'gx', 'gy'), may hold values from -12 to 12
- labels: int32 [128, 32, 256], P('gx', 'gy'), may hold values 0 or 1
Outputs:
- solution: float32 [3, 128, 32, 256], P(None, 'gx', 'gy')
- residual: float32 [3, 128, 32, 256], P(None, 'gx', 'gy')
All inputs are finite; a program needn't handle non-finite values. No bound on the sum of `labels` on one device may be relied on, other than what follows from the above.
Results may differ from a plain program's by a relative error of at most 0.0003.
Values sent between devices are 32-bit elements; how exact they have to be, the bound alone decides.
No kernel may reach another device: no remote copies, remote signals or barrier semaphores. Data moves between devices by JAX's collectives and lax.ppermute only.
A program may use at most 64 MiB of HBM per device.

v0:
```python
import math

import jax
import jax.numpy as jnp
import numpy as np
from jax import lax
from jax.sharding import PartitionSpec as P

ITERS = 4


LAMBDA_SOFT = 0.5769231
LAMBDA_RISE = 1.6452991
SHEAR_SOFT = 0.3846154
SHEAR_RISE = 2.9487179
KAPPA = 0.05


def shifted(shard, axis, by):
    size = lax.axis_size(axis)
    return lax.ppermute(shard, axis, [(i, (i + by) % size) for i in range(size)])


def corner_bits(corner):
    return (corner >> 2 & 1, corner >> 1 & 1, corner & 1)


def element_tables():
    gauss_offset = 0.5 / math.sqrt(3.0)
    gauss_points = [0.5 - gauss_offset, 0.5 + gauss_offset]
    lame_table = np.zeros((24, 24))
    shear_table = np.zeros((24, 24))
    normal_block = np.zeros((6, 6))
    normal_block[:3, :3] = 1.0
    shear_block = np.zeros((6, 6))
    for entry in range(6):
        shear_block[entry, entry] = 2.0 if entry < 3 else 1.0
    for point_x in gauss_points:
        for point_y in gauss_points:
            for point_z in gauss_points:
                strain = np.zeros((6, 24))
                for corner in range(8):
                    cx_bit, cy_bit, cz_bit = corner_bits(corner)
                    shape_x = point_x if cx_bit else 1.0 - point_x
                    shape_y = point_y if cy_bit else 1.0 - point_y
                    shape_z = point_z if cz_bit else 1.0 - point_z
                    slope_x = 1.0 if cx_bit else -1.0
                    slope_y = 1.0 if cy_bit else -1.0
                    slope_z = 1.0 if cz_bit else -1.0
                    grad_x = slope_x * shape_y * shape_z
                    grad_y = shape_x * slope_y * shape_z
                    grad_z = shape_x * shape_y * slope_z
                    column = 3 * corner
                    strain[0, column] = grad_x
                    strain[1, column + 1] = grad_y
                    strain[2, column + 2] = grad_z
                    strain[3, column + 1] = grad_z
                    strain[3, column + 2] = grad_y
                    strain[4, column] = grad_z
                    strain[4, column + 2] = grad_x
                    strain[5, column] = grad_y
                    strain[5, column + 1] = grad_x
                lame_table += 0.125 * strain.T @ normal_block @ strain
                shear_table += 0.125 * strain.T @ shear_block @ strain
    return np.concatenate([lame_table, shear_table], 0).astype(np.float32)


def table_diagonal(table):
    return np.array([table[entry, entry] for entry in range(24)], dtype=np.float32)


def moduli(labels):
    stiff = labels.astype(jnp.float32)
    return (LAMBDA_SOFT + LAMBDA_RISE * stiff, SHEAR_SOFT + SHEAR_RISE * stiff)


def element_terms(node_values, lame_block, shear_part, stiffness):
    planes, columns, depth = lame_block.shape
    rolled_z = jnp.roll(node_values, -1, 3)
    corner_views = []
    for corner in range(8):
        cx_bit, cy_bit, cz_bit = corner_bits(corner)
        source_nodes = rolled_z if cz_bit else node_values
        corner_views.append(source_nodes[:, cx_bit : cx_bit + planes, cy_bit : cy_bit + columns, :])
    stacked = jnp.concatenate(corner_views, 0).reshape(24, -1)
    products = jnp.dot(
        stiffness, stacked, precision=lax.Precision.HIGHEST, preferred_element_type=jnp.float32
    )
    forces = lame_block.reshape(1, -1) * products[:24] + shear_part.reshape(1, -1) * products[24:]
    return forces.reshape(8, 3, planes, columns, depth)


def diagonal_terms(lame_block, shear_part, diag_lame, diag_shear):
    planes, columns, depth = lame_block.shape
    forces = (
        lame_block[None] * diag_lame[:, None, None, None]
        + shear_part[None] * diag_shear[:, None, None, None]
    )
    return forces.reshape(8, 3, planes, columns, depth)


def assemble_corners(forces):
    assembled = None
    for corner in range(8):
        cx_bit, cy_bit, cz_bit = corner_bits(corner)
        portion = forces[corner]
        if cz_bit:
            portion = jnp.roll(portion, 1, 3)
        portion = jnp.pad(portion, ((0, 0), (cx_bit, 1 - cx_bit), (cy_bit, 1 - cy_bit), (0, 0)))
        assembled = portion if assembled is None else assembled + portion
    return assembled


def sweep_blocks(block_nodes, first_plane, block_count, block_width):

    def advance(carry, number):
        portion = block_nodes(number * block_width, block_width)
        portion = portion.at[:, 0].add(carry)
        return (portion[:, block_width], portion[:, :block_width])

    last_plane, pieces = lax.scan(advance, first_plane, jnp.arange(block_count, dtype=jnp.int32))
    assembled = jnp.moveaxis(pieces, 0, 1)
    assembled = assembled.reshape((3, block_count * block_width) + assembled.shape[3:])
    return (assembled, last_plane)


def fold_back(assembled, last_plane):
    arrived = shifted(last_plane, "gx", 1)
    assembled = assembled.at[:, 0].add(arrived)
    edge_index = assembled.shape[2] - 1
    column_in = shifted(assembled[:, :, edge_index], "gy", 1)
    assembled = assembled.at[:, :, 0].add(column_in)
    return assembled[:, :, :edge_index]


def owned_nodes(terms, block_count, block_width, plane_shape):

    def block_nodes(offset, planes):
        return assemble_corners(terms(offset, planes))

    first_plane = jnp.zeros(plane_shape, jnp.float32)
    assembled, last_plane = sweep_blocks(block_nodes, first_plane, block_count, block_width)
    return fold_back(assembled, last_plane)


def descent_sum(residual, scaled):
    return lax.psum(jnp.sum(residual * scaled), ("gx", "gy"))


def local(right_side, labels):
    tables = element_tables()
    stiffness = jnp.asarray(tables, dtype=jnp.float32)
    diag_lame = jnp.asarray(table_diagonal(tables[:24]), dtype=jnp.float32)
    diag_shear = jnp.asarray(table_diagonal(tables[24:]), dtype=jnp.float32)
    count_x = right_side.shape[1]
    count_y = right_side.shape[2]
    depth = right_side.shape[3]
    block_width = math.gcd(count_x, 4)
    block_count = count_x // block_width
    lame_first, shear_modulus = moduli(labels)
    plane_shape = (3, count_y + 1, depth)

    def diag_block(offset, planes):
        return diagonal_terms(
            lax.dynamic_slice_in_dim(lame_first, offset, planes, 0),
            lax.dynamic_slice_in_dim(shear_modulus, offset, planes, 0),
            diag_lame,
            diag_shear,
        )

    diagonal = owned_nodes(diag_block, block_count, block_width, plane_shape) + KAPPA
    solution = jnp.zeros_like(right_side)
    residual = right_side
    scaled = residual / diagonal
    direction = scaled
    descent = descent_sum(residual, scaled)
    for iteration in range(ITERS):
        upper_plane = shifted(direction[:, :1], "gx", -1)
        extended = jnp.concatenate([direction, upper_plane], 1)
        upper_column = shifted(extended[:, :, :1], "gy", -1)
        extended = jnp.concatenate([extended, upper_column], 2)

        def force_block(offset, planes):
            return element_terms(
                lax.dynamic_slice_in_dim(extended, offset, planes + 1, 1),
                lax.dynamic_slice_in_dim(lame_first, offset, planes, 0),
                lax.dynamic_slice_in_dim(shear_modulus, offset, planes, 0),
                stiffness,
            )

        image_vector = (
            owned_nodes(force_block, block_count, block_width, plane_shape) + KAPPA * direction
        )
        curve = lax.psum(jnp.sum(direction * image_vector), ("gx", "gy"))
        step_length = descent / curve
        solution = solution + step_length * direction
        residual = residual - step_length * image_vector
        if iteration + 1 < ITERS:
            scaled = residual / diagonal
            descent_new = descent_sum(residual, scaled)
            direction = scaled + descent_new / descent * direction
            descent = descent_new
    return (solution, residual)


def solution(mesh):
    in_specs = (P(None, "gx", "gy", None), P("gx", "gy", None))
    out_specs = (P(None, "gx", "gy", None), P(None, "gx", "gy", None))
    return jax.shard_map(local, mesh=mesh, in_specs=in_specs, out_specs=out_specs, check_vma=False)
```

profile of v0, /device:TPU:0, one launch (start us, length us, event | category | flops | bytes accessed | tf_op | source)
XLA Modules:
  0.0 497.5 jit_solution(1301822050732928141)
XLA Ops:
  1.6 11.0 %while.90 = (s32[]{:T(128)}, f32[3,9,256]{2,1,0:T(8,128)S(1)}, f32[4,3,4,9,256]{4,3,1,2,0:T(8,128)S(1)}, s32[4]{0:T(128)S(1)}, f32[16,8,256]{2,1,0:T(8,128)S(1)}...) while((s32[]{:T(128)}, f32[3,9,256]{2,1,0:T(8,128)S(1)}, ...), condition=%wide.region_1.2_spmd.clone, body=%wide.region_0.1_spmd.sunk.clone.sunk | while | flops 297990 | bytes 1946535 | solution.py:121
  13.5 4.3 collective-permute-done
  17.9 2.4 collective-permute-start.1
  20.3 4.1 collective-permute-done.1
  24.7 1.5 collective-permute-done.2
  26.2 2.0 collective-permute-start.3
  28.2 3.1 collective-permute-done.3
  32.4 23.3 %while.91 = (s32[]{:T(128)}, f32[3,9,256]{2,1,0:T(8,128)S(1)}, f32[4,3,4,9,256]{4,3,2,1,0:T(8,128)}, s32[4]{0:T(128)S(1)}, f32[16,8,256]{2,1,0:T(8,128)S(1)}, /*...) while((s32[]{:T(128)}, f32[3,9,256]{2,1,0:T(8,128)S(1)}, ...), condition=%wide.region_5.6_spmd.clone, body=%wide.region_4.5_spmd.sunk.clone.sunk | while | flops 115150856 | bytes 15201548 | solution.py:121
  35.0 1.4 fusion.152
  40.8 1.4 fusion.152
  46.6 1.4 fusion.152
  52.4 1.4 fusion.152
  55.9 1.4 copy.42
  57.5 2.6 collective-permute-done.4
  60.3 5.9 %collective-permute-done.5 = f32[3,16,256]{2,1,0:T(8,128)S(1)} collective-permute-done((f32[3,16,256]{2,1,0:T(8,128)S(1)}, f32[3,16,256]{2,1,0:T(8,128)S(1)}, u32[]{:S(2)}, u32[]{:S(2)}) %collective-permute-start.5) | collective-permute-done | bytes 49184 | tf_op jit(solution)/shard_map/ppermute | solution.py:21
  67.0 37.3 %all-reduce.40 = (f32[]{:T(128)}, f32[]{:T(128)}) all-reduce(f32[]{:T(128)} %get-tuple-element.869, f32[]{:T(128)} %get-tuple-element.868), channel_id=1, replica_groups=mesh['gx'=8,'gy'=4] {'gx','gy'}, use_global_device_ids=true, to_apply=%region_3.4 | all-reduce | flops 2 | bytes 16 | tf_op jit(solution)/shard_map/psum | solution.py:147
  106.6 42.3 %psum.58 = f32[]{:T(128)} all-reduce(f32[]{:T(128)} %get-tuple-element.944), channel_id=1, replica_groups=mesh['gx'=8,'gy'=4] {'gx','gy'}, use_global_device_ids=true, to_apply=%region_9.10 | all-reduce | flops 1 | bytes 8 | tf_op jit(solution)/shard_map/psum | solution.py:147
  151.6 1.5 collective-permute-done.6
  153.1 1.8 collective-permute-start.7
  154.9 2.8 collective-permute-done.7
  158.8 26.3 %while.92 = (s32[]{:T(128)}, f32[3,9,256]{2,1,0:T(8,128)S(1)}, f32[4,3,4,9,256]{4,3,2,1,0:T(8,128)}, s32[4]{0:T(128)S(1)}, f32[16,8,256]{2,1,0:T(8,128)S(1)}, /*...) while((s32[]{:T(128)}, f32[3,9,256]{2,1,0:T(8,128)S(1)}, ...), condition=%wide.region_11.12_spmd.clone, body=%wide.region_10.11_spmd.sunk.clone.sunk | while | flops 115150856 | bytes 17298812 | solution.py:121
  161.3 1.4 fusion.164
  167.9 1.4 fusion.164
  174.5 1.4 fusion.164
  181.1 1.4 fusion.164
  185.6 1.5 copy.46
  187.2 2.3 collective-permute-done.8
  189.8 5.9 %collective-permute-done.9 = f32[3,16,256]{2,1,0:T(8,128)S(1)} collective-permute-done((f32[3,16,256]{2,1,0:T(8,128)S(1)}, f32[3,16,256]{2,1,0:T(8,128)S(1)}, u32[]{:S(2)}, u32[]{:S(2)}) %collective-permute-start.9) | collective-permute-done | bytes 49184 | tf_op jit(solution)/shard_map/ppermute | solution.py:21
  196.4 37.3 %psum.59 = f32[]{:T(128)} all-reduce(f32[]{:T(128)} %multiply_reduce_fusion.4), channel_id=1, replica_groups=mesh['gx'=8,'gy'=4] {'gx','gy'}, use_global_device_ids=true, to_apply=%region_13.14 | all-reduce | flops 1 | bytes 8 | tf_op jit(solution)/shard_map/psum | solution.py:194
  235.8 42.7 %psum.60 = f32[]{:T(128)} all-reduce(f32[]{:T(128)} %get-tuple-element.942), channel_id=1, replica_groups=mesh['gx'=8,'gy'=4] {'gx','gy'}, use_global_device_ids=true, to_apply=%region_15.16 | all-reduce | flops 1 | bytes 8 | tf_op jit(solution)/shard_map/psum | solution.py:147
  281.1 1.5 collective-permute-done.10
  282.6 1.8 collective-permute-start.11
  284.4 3.0 collective-permute-done.11
  288.5 26.8 %while.93 = (s32[]{:T(128)}, f32[3,9,256]{2,1,0:T(8,128)S(1)}, f32[4,3,4,9,256]{4,3,2,1,0:T(8,128)}, s32[4]{0:T(128)S(1)}, f32[16,8,256]{2,1,0:T(8,128)S(1)}, /*...) while((s32[]{:T(128)}, f32[3,9,256]{2,1,0:T(8,128)S(1)}, ...), condition=%wide.region_17.18_spmd.clone, body=%wide.region_16.17_spmd.sunk.clone.sunk | while | flops 115150856 | bytes 17298812 | solution.py:121
  297.9 1.4 fusion.176
  315.5 1.5 copy.49
  317.2 2.5 collective-permute-done.12
  320.0 5.9 %collective-permute-done.13 = f32[3,16,256]{2,1,0:T(8,128)S(1)} collective-permute-done((f32[3,16,256]{2,1,0:T(8,128)S(1)}, f32[3,16,256]{2,1,0:T(8,128)S(1)}, u32[]{:S(2)}, u32[]{:S(2)}) %collective-permute-start.13) | collective-permute-done | bytes 49184 | tf_op jit(solution)/shard_map/ppermute | solution.py:21
  326.6 37.4 %psum.61 = f32[]{:T(128)} all-reduce(f32[]{:T(128)} %multiply_reduce_fusion.2), channel_id=1, replica_groups=mesh['gx'=8,'gy'=4] {'gx','gy'}, use_global_device_ids=true, to_apply=%region_19.20 | all-reduce | flops 1 | bytes 8 | tf_op jit(solution)/shard_map/psum | solution.py:194
  366.1 42.0 %psum.62 = f32[]{:T(128)} all-reduce(f32[]{:T(128)} %get-tuple-element.940), channel_id=1, replica_groups=mesh['gx'=8,'gy'=4] {'gx','gy'}, use_global_device_ids=true, to_apply=%region_21.22 | all-reduce | flops 1 | bytes 8 | tf_op jit(solution)/shard_map/psum | solution.py:147
  410.9 1.5 collective-permute-done.14
  412.4 1.8 collective-permute-start.15
  414.2 3.0 collective-permute-done.15
  418.3 26.9 %while.94 = (s32[]{:T(128)}, f32[3,9,256]{2,1,0:T(8,128)S(1)}, f32[4,3,4,9,256]{4,3,2,1,0:T(8,128)}, s32[4]{0:T(128)S(1)}, f32[16,8,256]{2,1,0:T(8,128)S(1)}, /*...) while((s32[]{:T(128)}, f32[3,9,256]{2,1,0:T(8,128)S(1)}, ...), condition=%wide.region_23.24_spmd.clone, body=%wide.region_22.23_spmd.sunk.clone.sunk | while | flops 115150856 | bytes 17298812 | solution.py:121
  445.5 1.5 copy.52
  447.2 2.5 collective-permute-done.16
  449.9 5.9 %collective-permute-done.17 = f32[3,16,256]{2,1,0:T(8,128)S(1)} collective-permute-done((f32[3,16,256]{2,1,0:T(8,128)S(1)}, f32[3,16,256]{2,1,0:T(8,128)S(1)}, u32[]{:S(2)}, u32[]{:S(2)}) %collective-permute-start.17) | collective-permute-done | bytes 49184 | tf_op jit(solution)/shard_map/ppermute | solution.py:21
  456.6 37.3 %psum.63 = f32[]{:T(128)} all-reduce(f32[]{:T(128)} %multiply_reduce_fusion), channel_id=1, replica_groups=mesh['gx'=8,'gy'=4] {'gx','gy'}, use_global_device_ids=true, to_apply=%region_25.26 | all-reduce | flops 1 | bytes 8 | tf_op jit(solution)/shard_map/psum | solution.py:194
  (860 shorter events, 106.2 us)
Async XLA Ops:
  12.6 11.8 %copy-start.22 = (f32[3,16,8,256]{3,2,1,0:T(8,128)S(1)}, f32[3,16,8,256]{3,2,1,0:T(8,128)}, u32[]{:S(2)}) copy-start(f32[3,16,8,256]{3,2,1,0:T(8,128)} %param.45) | copy-start | bytes 1179652
  12.7 5.1 %collective-permute-start = (f32[3,9,256]{2,0,1:T(4,128)S(1)}, f32[3,9,256]{2,0,1:T(4,128)S(1)}, u32[]{:S(2)}, u32[]{:S(2)}) collective-permute-start(f32[3,9,256]{2,0,1:T(4,128)S(1)} %copy.38), channel_id=1, source_target_pairs={{0,4},{4,8},{8,12},{12,16},{16,20},{20,24},{24,28},{28,0},{1,5},{5... | collective-permute-start | bytes 82952 | tf_op jit(solution)/shard_map/ppermute | solution.py:21
  17.9 6.5 %collective-permute-start.1 = (f32[3,16,256]{2,1,0:T(8,128)S(1)}, f32[3,16,256]{2,1,0:T(8,128)S(1)}, u32[]{:S(2)}, u32[]{:S(2)}) collective-permute-start(f32[3,16,256]{2,1,0:T(8,128)S(1)} %slice_bitcast_fusion.15), channel_id=1, source_target_pairs={{0,1},{1,2},{2,3},{3,0},{4,5},{5,6},{6,7},{7,4},{8,9},{9,10},{10,1... | collective-permute-start | bytes 147464 | tf_op jit(solution)/shard_map/ppermute | solution.py:21
  24.4 8.0 %copy-start.5 = (f32[48,24]{1,0:T(8,128)S(1)}, f32[48,24]{1,0:T(8,128)}, u32[]{:S(2)}) copy-start(f32[48,24]{1,0:T(8,128)} %constant.564.clone..sunk.8) | copy-start | bytes 13828
  24.6 1.6 collective-permute-start.2
  26.2 5.1 %collective-permute-start.3 = (f32[3,17,1,256]{3,1,0,2:T(8,128)S(1)}, f32[3,17,1,256]{3,1,0,2:T(8,128)S(1)}, u32[]{:S(2)}, u32[]{:S(2)}) collective-permute-start(f32[3,17,1,256]{3,1,0,2:T(8,128)S(1)} %pad_maximum_fusion.12), channel_id=1, source_target_pairs={{0,3},{1,0},{2,1},{3,2},{4,7},{5,4},{6,5},{7,6},{8,11},{9,8},{10,9... | collective-permute-start | bytes 156680 | tf_op jit(solution)/shard_map/ppermute | solution.py:21
  55.7 10.5 %copy-start.23 = (f32[3,16,8,256]{3,2,1,0:T(8,128)S(1)}, f32[3,16,8,256]{3,2,1,0:T(8,128)}, u32[]{:S(2)}) copy-start(f32[3,16,8,256]{3,2,1,0:T(8,128)} %param.45) | copy-start | bytes 1179652
  55.7 4.3 collective-permute-start.4
  60.3 5.9 %collective-permute-start.5 = (f32[3,16,256]{2,1,0:T(8,128)S(1)}, f32[3,16,256]{2,1,0:T(8,128)S(1)}, u32[]{:S(2)}, u32[]{:S(2)}) collective-permute-start(f32[3,16,256]{2,1,0:T(8,128)S(1)} %slice_bitcast_fusion.14), channel_id=1, source_target_pairs={{0,1},{1,2},{2,3},{3,0},{4,5},{5,6},{6,7},{7,4},{8,9},{9,10},{10,1... | collective-permute-start | bytes 147464 | tf_op jit(solution)/shard_map/ppermute | solution.py:21
  106.6 48.3 %copy-start.20 = (f32[3,16,8,256]{3,1,0,2:T(8,128)}, f32[3,16,8,256]{3,1,0,2:T(8,128)S(1)}, u32[]{:S(2)}) copy-start(f32[3,16,8,256]{3,1,0,2:T(8,128)S(1)} %get-tuple-element.945) | copy-start | bytes 1179652
  150.4 2.7 collective-permute-start.6
  153.1 4.6 collective-permute-start.7
  158.8 2.5 copy-start.12
  165.4 2.5 copy-start.12
  172.0 2.5 copy-start.12
  178.5 2.5 copy-start.12
  185.2 4.3 collective-permute-start.8
  185.6 49.4 %copy-start.21 = (f32[3,16,8,256]{3,1,0,2:T(8,128)S(1)}, f32[3,16,8,256]{3,1,0,2:T(8,128)}, u32[]{:S(2)}) copy-start(f32[3,16,8,256]{3,1,0,2:T(8,128)} %copy-done.20) | copy-start | bytes 1179652
  189.7 5.9 %collective-permute-start.9 = (f32[3,16,256]{2,1,0:T(8,128)S(1)}, f32[3,16,256]{2,1,0:T(8,128)S(1)}, u32[]{:S(2)}, u32[]{:S(2)}) collective-permute-start(f32[3,16,256]{2,1,0:T(8,128)S(1)} %slice_bitcast_fusion.13), channel_id=1, source_target_pairs={{0,1},{1,2},{2,3},{3,0},{4,5},{5,6},{6,7},{7,4},{8,9},{9,10},{10,1... | collective-permute-start | bytes 147464 | tf_op jit(solution)/shard_map/ppermute | solution.py:21
  235.8 51.8 %copy-start.18 = (f32[3,16,8,256]{3,1,0,2:T(8,128)}, f32[3,16,8,256]{3,1,0,2:T(8,128)S(1)}, u32[]{:S(2)}) copy-start(f32[3,16,8,256]{3,1,0,2:T(8,128)S(1)} %get-tuple-element.943) | copy-start | bytes 1179652
  279.9 8.7 %copy-start = (f32[3,16,8,256]{3,1,0,2:T(8,128)}, f32[3,16,8,256]{3,1,0,2:T(8,128)S(1)}, u32[]{:S(2)}) copy-start(f32[3,16,8,256]{3,1,0,2:T(8,128)S(1)} %multiply_add_fusion.3) | copy-start | bytes 1179652
  279.9 2.7 collective-permute-start.10
  282.6 4.8 collective-permute-start.11
  288.6 2.6 copy-start.14
  295.3 2.6 copy-start.14
  301.9 2.6 copy-start.14
  308.6 2.6 copy-start.14
  315.3 10.5 %copy-start.1 = (f32[3,16,8,256]{3,1,0,2:T(8,128)S(1)}, f32[3,16,8,256]{3,1,0,2:T(8,128)}, u32[]{:S(2)}) copy-start(f32[3,16,8,256]{3,1,0,2:T(8,128)} %copy-done) | copy-start | bytes 1179652
  315.3 4.3 collective-permute-start.12
  315.5 49.8 %copy-start.19 = (f32[3,16,8,256]{3,1,0,2:T(8,128)S(1)}, f32[3,16,8,256]{3,1,0,2:T(8,128)}, u32[]{:S(2)}) copy-start(f32[3,16,8,256]{3,1,0,2:T(8,128)} %copy-done.18) | copy-start | bytes 1179652
  319.9 5.9 %collective-permute-start.13 = (f32[3,16,256]{2,1,0:T(8,128)S(1)}, f32[3,16,256]{2,1,0:T(8,128)S(1)}, u32[]{:S(2)}, u32[]{:S(2)}) collective-permute-start(f32[3,16,256]{2,1,0:T(8,128)S(1)} %slice_bitcast_fusion.12), channel_id=1, source_target_pairs={{0,1},{1,2},{2,3},{3,0},{4,5},{5,6},{6,7},{7,4},{8,9},{9,10},{10,1... | collective-permute-start | bytes 147464 | tf_op jit(solution)/shard_map/ppermute | solution.py:21
  366.1 51.2 %copy-start.24 = (f32[3,16,8,256]{3,1,0,2:T(8,128)}, f32[3,16,8,256]{3,1,0,2:T(8,128)S(1)}, u32[]{:S(2)}) copy-start(f32[3,16,8,256]{3,1,0,2:T(8,128)S(1)} %get-tuple-element.941) | copy-start | bytes 1179652
  409.6 8.7 %copy-start.3 = (f32[3,16,8,256]{3,1,0,2:T(8,128)}, f32[3,16,8,256]{3,1,0,2:T(8,128)S(1)}, u32[]{:S(2)}) copy-start(f32[3,16,8,256]{3,1,0,2:T(8,128)S(1)} %multiply_add_fusion.2) | copy-start | bytes 1179652
  409.7 2.7 collective-permute-start.14
  412.4 4.8 collective-permute-start.15
  418.3 2.0 copy-start.10
  418.3 2.7 copy-start.16
  425.1 2.0 copy-start.10
  425.1 2.7 copy-start.16
  431.8 2.0 copy-start.10
  431.8 2.7 copy-start.16
  438.5 2.0 copy-start.10
  438.6 2.7 copy-start.16
  445.3 10.5 %copy-start.4 = (f32[3,16,8,256]{3,1,0,2:T(8,128)S(1)}, f32[3,16,8,256]{3,1,0,2:T(8,128)}, u32[]{:S(2)}) copy-start(f32[3,16,8,256]{3,1,0,2:T(8,128)} %copy-done.3) | copy-start | bytes 1179652
  445.3 4.3 collective-permute-start.16
  445.5 49.8 %copy-start.2 = (f32[3,16,8,256]{3,1,0,2:T(8,128)S(1)}, f32[3,16,8,256]{3,1,0,2:T(8,128)}, u32[]{:S(2)}) copy-start(f32[3,16,8,256]{3,1,0,2:T(8,128)} %copy-done) | copy-start | bytes 1179652
  445.5 49.8 %copy-start.25 = (f32[3,16,8,256]{3,1,0,2:T(8,128)S(1)}, f32[3,16,8,256]{3,1,0,2:T(8,128)}, u32[]{:S(2)}) copy-start(f32[3,16,8,256]{3,1,0,2:T(8,128)} %copy-done.24) | copy-start | bytes 1179652
  449.9 5.9 %collective-permute-start.17 = (f32[3,16,256]{2,1,0:T(8,128)S(1)}, f32[3,16,256]{2,1,0:T(8,128)S(1)}, u32[]{:S(2)}, u32[]{:S(2)}) collective-permute-start(f32[3,16,256]{2,1,0:T(8,128)S(1)} %slice_bitcast_fusion.11), channel_id=1, source_target_pairs={{0,1},{1,2},{2,3},{3,0},{4,5},{5,6},{6,7},{7,4},{8,9},{9,10},{10,1... | collective-permute-start | bytes 147464 | tf_op jit(solution)/shard_map/ppermute | solution.py:21
  (32 other events, 43.9 us)
where the time goes:
time: 500 us; the launch traced here: 498 us
  blocking collectives  276 us (55%)
  local copies, waits for them, and re-layouts  76.6 us (15%)
  waiting for transfers between devices  59.8 us (12%)
  matrix products  21.8 us (4%)
  other arithmetic  20.5 us (4%)
  loops' own time  16.7 us (3%)
  starting transfers between devices  15.2 us (3%)
  between operations  10.5 us (2%)
    psum x4, blocking collectives, descent_sum(): return lax.psum(jnp.sum(residual * scaled), ('gx', 'gy'))  164 us
    psum x3, blocking collectives, local(): curve = lax.psum(jnp.sum(direction * image_vector), ('gx', 'gy'))  112 us
    ppermute x18, waiting for transfers between devices, shifted(): lax.ppermute(shard, axis, [(i, (i + by) % size) for i in range(size)])  59.8 us
    while x384, local copies, waits for them, and re-layouts  22.8 us
    dot_general x16, matrix products, element_terms(): jnp.dot(stiffness, stacked, precision=lax.Precision.HIGHEST, preferred_el...  21.8 us
    another operation x5, loops' own time, sweep_blocks(): lax.scan(advance, first_plane, jnp.arange(block_count, dtype=jnp.int32))  16.7 us
    ppermute x18, starting transfers between devices, shifted(): lax.ppermute(shard, axis, [(i, (i + by) % size) for i in range(size)])  15.2 us
    dynamic_slice x20, local copies, waits for them, and re-layouts, sweep_blocks(): lax.scan(advance, first_plane, jnp.arange(block_count, dtype=jnp.int32))  12.4 us
  transfers between devices with their start and end apart: 18, of which 18 were waited for; matrix products, arithmetic and copies ran while one was open for 1% of the time, Pallas kernels for 0%

commit v1 on v0

v1 whole, which is shorter than its diff:
```python
import jax
import jax.numpy as jnp
from jax import lax
from jax.experimental import pallas as pl
from jax.experimental.pallas import tpu as pltpu
from jax.sharding import PartitionSpec as P

ITERS = 4
HALO = ITERS
LAMBDA_SOFT = 0.5769231
LAMBDA_RISE = 1.6452991
SHEAR_SOFT = 0.3846154
SHEAR_RISE = 2.9487179
KAPPA = 0.05
CENTRE = 0.5 * (0.5 + 2.6)
HALF = 0.5 * (2.6 - 0.5)
SUMS = 14


def shifted(shard, axis, by):
    size = lax.axis_size(axis)
    return lax.ppermute(shard, axis, [(i, (i + by) % size) for i in range(size)])


def roll(v, by, axis):
    return pltpu.roll(v, by % v.shape[axis], axis)


def gather_modes(v):
    ahead = roll(v, -1, 1)
    out = {}
    for bz, a in ((0, v + ahead), (1, ahead - v)):
        up = roll(a, -1, 0)
        out[0, bz] = a + up
        out[1, bz] = up - a
    return out


def scatter_modes(r):
    part = []
    for bz in (0, 1):
        part.append((r[0, bz] - r[1, bz]) + roll(r[0, bz] + r[1, bz], 1, 0))
    return (part[0] - part[1]) + roll(part[0] + part[1], 1, 1)


def voxel_forces(c, stiff):
    lam = (LAMBDA_SOFT / 16) + (LAMBDA_RISE / 16) * stiff
    mu = (SHEAR_SOFT / 16) + (SHEAR_RISE / 16) * stiff
    mu2 = mu + mu
    lam3 = lam * (1.0 / 3)
    mu3 = mu * (1.0 / 3)
    top = ((LAMBDA_SOFT + 4 * SHEAR_SOFT) / 144) + ((LAMBDA_RISE + 4 * SHEAR_RISE) / 144) * stiff
    f = {}
    normal = ((0, 1, 0, 0), (1, 0, 1, 0), (2, 0, 0, 1))
    t = lam * (c[normal[0]] + c[normal[1]] + c[normal[2]])
    for p in normal:
        f[p] = t + mu2 * c[p]
    for p, q in (
        ((0, 1, 1, 0), (2, 0, 1, 1)),
        ((0, 1, 0, 1), (1, 0, 1, 1)),
        ((1, 1, 1, 0), (2, 1, 0, 1)),
    ):
        t = lam3 * (c[p] + c[q])
        f[p] = t + mu * c[p]
        f[q] = t + mu * c[q]
    for comp in range(3):
        p = (comp, 1, 1, 1)
        f[p] = top * c[p]
    for p, q in (
        ((0, 0, 1, 0), (1, 1, 0, 0)),
        ((0, 0, 0, 1), (2, 1, 0, 0)),
        ((1, 0, 0, 1), (2, 0, 1, 0)),
    ):
        f[p] = f[q] = mu * (c[p] + c[q])
    bend = ((0, 0, 1, 1), (1, 1, 0, 1), (2, 1, 1, 0))
    t = c[bend[0]] + c[bend[1]] + c[bend[2]]
    for p in bend:
        f[p] = mu3 * (t + c[p])
    return f


MODES = [(comp, by, bz) for comp in range(3) for by in (0, 1) for bz in (0, 1)]


def basis_kernel(r_ref, lab_ref, edge_ref, t_out, d_out, sums_out, t_ref, inv_ref, q_ref, f_ref):
    planes, rows, depth = r_ref.shape[1:]
    own_x = planes - 2 * HALO
    own_y = rows - 2 * HALO
    lo, hi = HALO, HALO + own_x
    first_row = own_y + HALO

    base = 8 * (LAMBDA_SOFT + 4 * SHEAR_SOFT) / 9 + KAPPA
    rise = (LAMBDA_RISE + 4 * SHEAR_RISE) / 9
    row_id = lax.broadcasted_iota(jnp.int32, (rows, depth), 0)

    def layer(m):
        l = lab_ref[m]
        lz = l + roll(l, 1, 1)
        e = edge_ref[pl.ds(m, 1), :]
        ez = jnp.broadcast_to(e + roll(e, 1, 1), (rows, depth))
        return lz + jnp.where(row_id == first_row, ez, roll(lz, 1, 0))

    def start(n, before):
        here = layer(n + 1)
        diag = base + rise * (before + here)
        inv = 1.0 / diag
        inv_ref[n] = inv
        for comp in range(3):
            t_ref[0, comp, n] = r_ref[comp, n] * inv

        @pl.when((n >= lo) & (n < hi))
        def _():
            d_out[n - lo] = diag[:own_y]
            for comp in range(3):
                t_out[0, comp, n - lo] = t_ref[0, comp, n][:own_y]

        return here

    lax.fori_loop(0, planes, start, layer(0))

    tiles = [
        (slice(a, a + 8), slice(b, b + 128)) for a in range(0, rows, 8) for b in range(0, depth, 128)
    ]
    totals = []
    for k in range(ITERS):
        first, last = k, planes - k

        def forward(n, _):
            for comp in range(3):
                out = gather_modes(t_ref[k, comp, n])
                for i, (cc, by, bz) in enumerate(MODES):
                    if cc == comp:
                        q_ref[i, n] = out[by, bz]
            return _

        lax.fori_loop(first, last, forward, 0)

        for tile in tiles:

            def voxels(n, carry):
                near, behind = carry
                far = [q_ref[i, n + 1, tile[0], tile[1]] for i in range(len(MODES))]
                c = {}
                for i, (comp, by, bz) in enumerate(MODES):
                    if (by, bz) != (0, 0):
                        c[comp, 0, by, bz] = near[i] + far[i]
                    c[comp, 1, by, bz] = far[i] - near[i]
                f = voxel_forces(c, lab_ref[n + 1, tile[0], tile[1]])
                ahead = []
                for i, (comp, by, bz) in enumerate(MODES):
                    up = f[comp, 1, by, bz]
                    if (by, bz) != (0, 0):
                        flat = f[comp, 0, by, bz]
                        f_ref[i, n, tile[0], tile[1]] = behind[i] + (flat - up)
                        ahead.append(flat + up)
                    else:
                        f_ref[i, n, tile[0], tile[1]] = behind[i] - up
                        ahead.append(up)
                return far, ahead

            near = [q_ref[i, first, tile[0], tile[1]] for i in range(len(MODES))]
            lax.fori_loop(first, last - 1, voxels, (near, [jnp.zeros_like(v) for v in near]))

        def advance(n, own, acc):
            acc = list(acc)
            inv = inv_ref[n]
            for comp in range(3):
                modes = {
                    (by, bz): f_ref[i, n]
                    for i, (cc, by, bz) in enumerate(MODES)
                    if cc == comp
                }
                t = t_ref[k, comp, n]
                image = scatter_modes(modes) + KAPPA * t
                if own:
                    for j in range(k + 1):
                        acc[j] += t_ref[j, comp, n, :own_y] * image[:own_y]
                    acc[k + 1] += t[:own_y] * r_ref[comp, n, :own_y]
                new = image * inv
                if k == 1:
                    new = (new - CENTRE * t) * (1 / HALF)
                elif k > 1:
                    new = (new - CENTRE * t) * (2 / HALF) - t_ref[k - 1, comp, n]
                if k + 1 < ITERS:
                    t_ref[k + 1, comp, n] = new
                if own:
                    t_out[k + 1, comp, n - lo] = new[:own_y]
            return tuple(acc)

        if k + 1 < ITERS:
            lax.fori_loop(first + 1, lo, lambda n, c: advance(n, False, c), ())
            lax.fori_loop(hi, last - 1, lambda n, c: advance(n, False, c), ())
        zero = jnp.zeros((own_y, depth), jnp.float32)
        acc = lax.fori_loop(lo, hi, lambda n, c: advance(n, True, c), (zero,) * (k + 2))
        totals.extend(acc)

    lane = lax.broadcasted_iota(jnp.int32, (1, 128), 1)
    packed = jnp.zeros((1, 128), jnp.float32)
    for i, v in enumerate(totals):
        s = jnp.sum(jnp.sum(v, axis=0, keepdims=True), axis=1, keepdims=True)
        packed = jnp.where(lane == i, s, packed)
    sums_out[...] = packed


def combine_kernel(sums_ref, t_ref, d_ref, x_out, r_out):
    total = jnp.sum(sums_ref[...], axis=0, keepdims=True)
    lane = lax.broadcasted_iota(jnp.int32, total.shape, 1)
    entry = [
        jnp.sum(jnp.where(lane == i, total, 0.0), axis=1, keepdims=True) for i in range(SUMS)
    ]
    gram, right = {}, []
    place = 0
    for k in range(ITERS):
        for j in range(k + 1):
            gram[j, k] = gram[k, j] = entry[place]
            place += 1
        right.append(entry[place])
        place += 1
    scale = [gram[k, k] for k in range(ITERS)]
    inv, low = [], {}
    for k in range(ITERS):
        pivot = gram[k, k]
        good = pivot > 1e-7 * scale[k]
        inv.append(jnp.where(good, 1.0 / jnp.where(good, pivot, 1.0), 0.0))
        for i in range(k + 1, ITERS):
            low[i, k] = gram[i, k] * inv[k]
        for i in range(k + 1, ITERS):
            for j in range(k + 1, i + 1):
                gram[i, j] = gram[j, i] = gram[i, j] - low[i, k] * gram[j, k]
            right[i] = right[i] - low[i, k] * right[k]
    y = [None] * ITERS
    for k in reversed(range(ITERS)):
        y[k] = right[k] * inv[k]
        for i in range(k + 1, ITERS):
            y[k] = y[k] - low[i, k] * y[i]
    e = [jnp.ones_like(y[0])] + [jnp.zeros_like(y[0]) for _ in range(ITERS)]
    for k in range(ITERS):
        if k == 0:
            e[1] = e[1] - y[0]
        elif k == 1:
            e[2] = e[2] - HALF * y[1]
            e[1] = e[1] - CENTRE * y[1]
        else:
            e[k + 1] = e[k + 1] - (HALF / 2) * y[k]
            e[k - 1] = e[k - 1] - (HALF / 2) * y[k]
            e[k] = e[k] - CENTRE * y[k]
    shape = d_ref.shape[1:]
    y = [jnp.broadcast_to(v, shape) for v in y]
    e = [jnp.broadcast_to(v, shape) for v in e]

    def body(n, _):
        diag = d_ref[n]
        for comp in range(3):
            t = [t_ref[k, comp, n] for k in range(ITERS + 1)]
            x, r = y[0] * t[0], e[0] * t[0]
            for k in range(1, ITERS):
                x = x + y[k] * t[k]
                r = r + e[k] * t[k]
            r = r + e[ITERS] * t[ITERS]
            x_out[comp, n] = x
            r_out[comp, n] = r * diag
        return _

    lax.fori_loop(0, d_ref.shape[0], body, 0)


def local(right_side, labels):
    own_x, own_y, depth = labels.shape
    h = HALO
    devices = lax.axis_size("gx") * lax.axis_size("gy")
    lab = labels.astype(jnp.float32)
    both = jnp.concatenate([right_side, lab[None]], 0)

    to_plus = both[:, :, own_y - h :].reshape(4 * own_x, h, depth)
    edge_rows = lab[:, own_y - h - 1].reshape(own_x // h, h, depth)
    from_minus = shifted(jnp.concatenate([to_plus, edge_rows], 0), "gy", 1)
    from_plus = shifted(both[:, :, :h].reshape(4 * own_x, h, depth), "gy", -1)

    def to_next(block, voxels, extra):
        parts = [block[:, own_x - h :].reshape(3 * h, -1, depth), voxels[own_x - h - 1 :]]
        return shifted(jnp.concatenate(parts + extra, 0), "gx", 1)

    def to_previous(block, voxels, extra):
        parts = [block[:, :h].reshape(3 * h, -1, depth), voxels[:h]]
        return shifted(jnp.concatenate(parts + extra, 0), "gx", -1)

    below = to_next(right_side, lab, [])
    above = to_previous(right_side, lab, [])

    side = jnp.concatenate(
        [
            from_plus.reshape(4, own_x, h, depth),
            from_minus[: 4 * own_x].reshape(4, own_x, h, depth),
        ],
        2,
    )
    edge = from_minus[4 * own_x :].reshape(own_x, depth)
    side_r, side_l = side[:3], side[3]

    def padded(rows):
        return jnp.pad(rows, ((0, 2 * h - rows.shape[0]), (0, 0)))[None]

    below_side = to_next(side_r, side_l, [padded(edge[own_x - h - 1 :])])
    above_side = to_previous(side_r, side_l, [padded(edge[:h])])

    def extended(block, voxels, low, high):
        nodes = jnp.concatenate(
            [
                low[: 3 * h].reshape(3, h, -1, depth),
                block,
                high[: 3 * h].reshape(3, h, -1, depth),
            ],
            1,
        )
        cells = jnp.concatenate([low[3 * h : 4 * h + 1], voxels, high[3 * h : 4 * h]], 0)
        return nodes, cells

    nodes_a, cells_a = extended(right_side, lab, below, above)
    nodes_b, cells_b = extended(side_r, side_l, below_side, above_side)
    nodes = jnp.concatenate([nodes_a, nodes_b], 2)
    cells = jnp.concatenate([cells_a, cells_b], 1)
    edges = jnp.concatenate([below_side[4 * h + 1, : h + 1], edge, above_side[4 * h, :h]], 0)

    planes, rows = nodes.shape[1:3]
    f32 = jnp.float32
    basis, diagonal, sums = pl.pallas_call(
        basis_kernel,
        out_shape=(
            jax.ShapeDtypeStruct((ITERS + 1, 3, own_x, own_y, depth), f32),
            jax.ShapeDtypeStruct((own_x, own_y, depth), f32),
            jax.ShapeDtypeStruct((1, 128), f32),
        ),
        scratch_shapes=[
            pltpu.VMEM((ITERS, 3, planes, rows, depth), f32),
            pltpu.VMEM((planes, rows, depth), f32),
            pltpu.VMEM((len(MODES), planes, rows, depth), f32),
            pltpu.VMEM((len(MODES), planes, rows, depth), f32),
        ],
        name="basis",
    )(nodes, cells, edges)

    everyone = lax.all_to_all(
        jnp.broadcast_to(sums[None], (devices,) + sums.shape), ("gx", "gy"), 0, 0
    )
    out = jax.ShapeDtypeStruct(right_side.shape, f32)
    return pl.pallas_call(combine_kernel, out_shape=(out, out), name="combine")(
        everyone.reshape(devices, 128), basis, diagonal
    )


def solution(mesh):
    in_specs = (P(None, "gx", "gy", None), P("gx", "gy", None))
    out_specs = (P(None, "gx", "gy", None), P(None, "gx", "gy", None))
    return jax.shard_map(local, mesh=mesh, in_specs=in_specs, out_specs=out_specs, check_vma=False)
```

time: 500 us -> 70.6 us (0.14)
  blocking collectives: 276 us -> 9.57 us
  local copies, waits for them, and re-layouts: 76.6 us -> 0.85 us
  waiting for transfers between devices: 59.8 us -> 15.2 us
  Pallas kernels: 0 us -> 29.8 us
  matrix products: 21.8 us -> 0 us
  loops' own time: 16.7 us -> 0 us
  other arithmetic: 20.5 us -> 5 us
  between operations: 10.5 us -> 0.92 us
  starting transfers between devices: 15.2 us -> 9.06 us
    psum x7 -> x0, blocking collectives: 276 us -> none  [the longest x4 164 us: descent_sum(): return lax.psum(jnp.sum(residual * scaled), ('gx', 'gy'))]
    ppermute x18 -> x6, waiting for transfers between devices: 59.8 us -> 15.2 us  [shifted(): lax.ppermute(shard, axis, [(i, (i + by) % size) for i in range(size)])]
    pallas_call x0 -> x2, Pallas kernels: none -> 29.8 us  [the longest x1 27 us: local(): pl.pallas_call(basis_kernel, out_shape=(jax.ShapeDtypeStruct((ITERS + 1,...]
    while x389 -> x0, local copies, waits for them, and re-layouts: 22.9 us -> none
    dot_general x16 -> x0, matrix products: 21.8 us -> none  [element_terms(): jnp.dot(stiffness, stacked, precision=lax.Precision.HIGHEST, preferred_el...]
    another operation x5 -> x0, loops' own time: 16.7 us -> none  [sweep_blocks(): lax.scan(advance, first_plane, jnp.arange(block_count, dtype=jnp.int32))]
    dynamic_slice x32 -> x0, local copies, waits for them, and re-layouts: 14.3 us -> none  [the longest x20 12.4 us: sweep_blocks(): lax.scan(advance, first_plane, jnp.arange(block_count, dtype=jnp.int32))]
    slice x148 -> x20, local copies, waits for them, and re-layouts: 13.6 us -> 0.15 us  [the longest x1 0.05 us: local(): edge_rows = lab[:, own_y - h - 1].reshape(own_x // h, h, depth)]
  transfers between devices with their start and end apart: 18 -> 6, of which waited for: 18 -> 5; matrix products, arithmetic and copies ran while one was open for 1% -> 0% of each run, Pallas kernels for 0% -> 0%
where the time goes in v1:
time: 70.6 us; the launch traced here: 70.4 us
  Pallas kernels  29.8 us (42%)
  waiting for transfers between devices  15.2 us (22%)
  blocking collectives  9.57 us (14%)
  starting transfers between devices  9.06 us (13%)
  other arithmetic  5 us (7%)
  between operations  0.92 us (1%)
  local copies, waits for them, and re-layouts  0.85 us (1%)
    pallas_call x1, Pallas kernels, local(): pl.pallas_call(basis_kernel, out_shape=(jax.ShapeDtypeStruct((ITERS + 1,...  27 us
    ppermute x6, waiting for transfers between devices, shifted(): lax.ppermute(shard, axis, [(i, (i + by) % size) for i in range(size)])  15.2 us
    all_to_all x1, blocking collectives, local(): lax.all_to_all(jnp.broadcast_to(sums[None], (devices,) + sums.shape), ('g...  9.57 us
    ppermute x6, starting transfers between devices, shifted(): lax.ppermute(shard, axis, [(i, (i + by) % size) for i in range(size)])  9.06 us
    pallas_call x1, Pallas kernels, local(): pl.pallas_call(combine_kernel, out_shape=(out, out), name='combine')  2.85 us
  transfers between devices with their start and end apart: 6, of which 5 were waited for; matrix products, arithmetic and copies ran while one was open for 0% of the time, Pallas kernels for 0%

profile of v1, /device:TPU:0, one launch (start us, length us, event | category | flops | bytes accessed | tf_op | source)
XLA Modules:
  0.0 70.4 jit_solution(16674164417617115764)
XLA Ops:
  0.6 0.0 copy-start
  0.6 1.0 %convert_bitcast_fusion = (f32[1,16,8,256]{3,2,1,0:T(8,128)S(1)}, f32[16,8,256]{2,1,0:T(8,128)S(1)}) fusion(s32[16,8,256]{2,1,0:T(8,128)} %param.3), kind=kLoop, calls=%fused_computation.37 | loop fusion | flops 32768 | bytes 393216 | tf_op jit(solution)/shard_map/broadcast_in_dim | solution.py:272
  1.6 1.2 %fusion.1 = (f32[4,16,4,256]{3,2,1,0:T(4,128)S(1)}, f32[4,16,4,256]{3,2,1,0:T(4,128)S(1)}) fusion(f32[3,16,8,256]{3,2,1,0:T(8,128)} %param.2, f32[1,16,8,256]{3,2,1,0:T(8,128)S(1)} %get-tuple-element.14), kind=kLoop, calls=%fused_computation.16 | loop fusion | flops 131072 | bytes 1048576 | tf_op jit(solution)/shard_map/concatenate | solution.py:272
  2.8 5.1 %collective-permute-start.2 = (f32[64,4,256]{2,1,0:T(4,128)S(1)}, f32[64,4,256]{2,1,0:T(4,128)S(1)}, u32[]{:S(2)}, u32[]{:S(2)}) collective-permute-start(f32[64,4,256]{2,1,0:T(4,128)S(1)} %bitcast.51), channel_id=1, source_target_pairs={{0,3},{1,0},{2,1},{3,2},{4,7},{5,4},{6,5},{7,6},{8,11},{9,8},{10,9... | collective-permute-start | bytes 786440 | tf_op jit(solution)/shard_map/ppermute | solution.py:22
  8.0 0.1 pad_maximum_fusion
  8.1 0.1 collective-permute-start.3
  8.2 0.0 copy-done
  8.2 0.1 collective-permute-start
  8.3 2.7 %collective-permute-start.1 = (f32[16,8,256]{2,1,0:T(8,128)S(1)}, f32[16,8,256]{2,1,0:T(8,128)S(1)}, u32[]{:S(2)}, u32[]{:S(2)}) collective-permute-start(f32[16,8,256]{2,1,0:T(8,128)S(1)} %pad_maximum_fusion.6), channel_id=1, source_target_pairs={{0,28},{4,0},{8,4},{12,8},{16,12},{20,16},{24,20},{28,24},{1,29},{... | collective-permute-start | bytes 393224 | tf_op jit(solution)/shard_map/ppermute | solution.py:22
  11.0 2.5 %collective-permute-done.1 = f32[16,8,256]{2,1,0:T(8,128)S(1)} collective-permute-done((f32[16,8,256]{2,1,0:T(8,128)S(1)}, f32[16,8,256]{2,1,0:T(8,128)S(1)}, u32[]{:S(2)}, u32[]{:S(2)}) %collective-permute-start.1) | collective-permute-done | bytes 131104 | tf_op jit(solution)/shard_map/ppermute | solution.py:22
  13.5 0.0 copy-start.1
  13.5 0.1 collective-permute-done
  13.7 0.0 copy-start.2
  13.7 6.7 %collective-permute-done.3 = f32[68,4,256]{2,1,0:T(4,128)S(1)} collective-permute-done((f32[68,4,256]{2,1,0:T(4,128)S(1)}, f32[68,4,256]{2,1,0:T(4,128)S(1)}, u32[]{:S(2)}, u32[]{:S(2)}) %collective-permute-start.3) | collective-permute-done | bytes 278560 | tf_op jit(solution)/shard_map/ppermute | solution.py:22
  20.4 0.0 collective-permute-done.2
  20.5 0.0 copy-done.1
  20.5 0.0 copy-done.2
  20.6 0.0 slice-start
  20.6 0.0 slice-start.2
  20.7 1.1 %collective-permute-start.5 = (f32[17,8,256]{2,1,0:T(8,128)S(1)}, f32[17,8,256]{2,1,0:T(8,128)S(1)}, u32[]{:S(2)}, u32[]{:S(2)}) collective-permute-start(f32[17,8,256]{2,1,0:T(8,128)S(1)} %pad_maximum_fusion.4), channel_id=1, source_target_pairs={{0,28},{4,0},{8,4},{12,8},{16,12},{20,16},{24,20},{28,24},{1,29},{... | collective-permute-start | bytes 417800 | tf_op jit(solution)/shard_map/ppermute | solution.py:22
  21.8 0.0 slice-start.1
  21.8 0.0 slice-start.3
  21.8 0.1 collective-permute-start.4
  21.9 0.1 fusion
  22.0 3.8 %collective-permute-done.5 = f32[17,8,256]{2,1,0:T(8,128)S(1)} collective-permute-done((f32[17,8,256]{2,1,0:T(8,128)S(1)}, f32[17,8,256]{2,1,0:T(8,128)S(1)}, u32[]{:S(2)}, u32[]{:S(2)}) %collective-permute-start.5) | collective-permute-done | bytes 139296 | tf_op jit(solution)/shard_map/ppermute | solution.py:22
  25.8 2.0 %collective-permute-done.4 = f32[18,8,256]{2,1,0:T(8,128)S(1)} collective-permute-done((f32[18,8,256]{2,1,0:T(8,128)S(1)}, f32[18,8,256]{2,1,0:T(8,128)S(1)}, u32[]{:S(2)}, u32[]{:S(2)}) %collective-permute-start.4) | collective-permute-done | bytes 147488 | tf_op jit(solution)/shard_map/ppermute | solution.py:22
  27.8 0.6 pad_maximum_fusion.7.edge_ref
  28.4 0.0 slice-done
  28.4 0.0 slice-done.2
  28.4 0.8 %maximum_maximum_fusion.1.lab_ref = f32[25,16,256]{2,1,0:T(8,128)} fusion(f32[4,8,256]{2,1,0:T(8,128)S(1)} %slice.151, f32[16,8,256]{2,1,0:T(8,128)S(1)} %fusion.2, f32[5,8,256]{2,1,0:T(8,128)S(1)} %slice.150, f32[4,8,256]{2,1,0:T(8,128)S(1)} %slice-done, f32[16,8,256]{2,1,0:T(8,128)S(1)} %get-tuple-element.15, f32[5,8,256]{2,1,0:T(8,128)S(1)} %slice-done.2), kind=kLoop, calls=%fused_computation.13 | loop fusion | flops 512000 | bytes 819200 | tf_op jit(solution)/shard_map/concatenate | solution.py:321
  29.2 0.0 slice-done.1
  29.2 0.0 slice-done.3
  29.2 1.1 %maximum_maximum_fusion.r_ref = f32[3,24,16,256]{3,2,1,0:T(8,128)} fusion(f32[3,4,8,256]{3,2,1,0:T(8,128)S(1)} %bitcast.45, f32[3,16,8,256]{3,2,1,0:T(8,128)S(1)} %fusion, f32[3,4,8,256]{3,2,1,0:T(8,128)S(1)} %bitcast.46, f32[3,4,8,256]{3,2,1,0:T(8,128)S(1)} %bitcast.43, f32[3,16,8,256]{3,2,1,0:T(8,128)S(1)} %copy-done, f32[3,4,8,256]{3,2,1,0:T(8,128)S(1)} %bitcast.44), kind=kLoop, calls=%fused_computation | loop fusion | flops 1474560 | bytes 2359296 | tf_op jit(solution)/shard_map/concatenate | solution.py:320
  30.3 27.0 %basis.1 = (f32[5,3,16,8,256]{4,3,2,1,0:T(8,128)}, f32[16,8,256]{2,1,0:T(8,128)}, f32[1,128]{1,0:T(1,128)}) custom-call(f32[3,24,16,256]{3,2,1,0:T(8,128)} %maximum_maximum_fusion.r_ref, f32[25,16,256]{2,1,0:T(8,128)} %maximum_maximum_fusion.1.lab_ref, f32[25,256]{1,0:T(8,128)} %pad_maximum_fusion.7.edge_ref), custom_call_target="tpu_custom_call" | custom-call | tf_op jit(solution)/shard_map/basis/pallas_call | solution.py:326
  57.3 0.7 broadcast_in_dim.21
  58.0 9.6 %all_to_all.5 = f32[32,1,128]{2,1,0:T(1,128)} all-to-all(f32[32,1,128]{2,1,0:T(1,128)S(1)} %broadcast_in_dim.21), channel_id=1, replica_groups=mesh['gx'=8,'gy'=4] {'gx','gy'}, dimensions={0} | all-to-all | bytes 32768 | tf_op jit(solution)/shard_map/all_to_all | solution.py:342
  67.5 2.9 %combine.1 = (f32[3,16,8,256]{3,2,1,0:T(8,128)}, f32[3,16,8,256]{3,2,1,0:T(8,128)}) custom-call(f32[32,128]{1,0:T(8,128)} %bitcast.52, f32[5,3,16,8,256]{4,3,2,1,0:T(8,128)} %get-tuple-element.6.t_ref, f32[16,8,256]{2,1,0:T(8,128)} %get-tuple-element.7.d_ref), custom_call_target="tpu_custom_call" | custom-call | tf_op jit(solution)/shard_map/combine/pallas_call | solution.py:346
  (26 shorter events, 0.3 us)
Async XLA Ops:
  0.6 7.5 %copy-start = (f32[3,16,8,256]{3,2,1,0:T(8,128)S(1)}, f32[3,16,8,256]{3,2,1,0:T(8,128)}, u32[]{:S(2)}) copy-start(f32[3,16,8,256]{3,2,1,0:T(8,128)} %param.2) | copy-start | bytes 1179652
  2.8 17.6 %collective-permute-start.2 = (f32[64,4,256]{2,1,0:T(4,128)S(1)}, f32[64,4,256]{2,1,0:T(4,128)S(1)}, u32[]{:S(2)}, u32[]{:S(2)}) collective-permute-start(f32[64,4,256]{2,1,0:T(4,128)S(1)} %bitcast.51), channel_id=1, source_target_pairs={{0,3},{1,0},{2,1},{3,2},{4,7},{5,4},{6,5},{7,6},{8,11},{9,8},{10,9... | collective-permute-start | bytes 786440 | tf_op jit(solution)/shard_map/ppermute | solution.py:22
  8.1 12.3 %collective-permute-start.3 = (f32[68,4,256]{2,1,0:T(4,128)S(1)}, f32[68,4,256]{2,1,0:T(4,128)S(1)}, u32[]{:S(2)}, u32[]{:S(2)}) collective-permute-start(f32[68,4,256]{2,1,0:T(4,128)S(1)} %pad_maximum_fusion), channel_id=1, source_target_pairs={{0,1},{1,2},{2,3},{3,0},{4,5},{5,6},{6,7},{7,4},{8,9},{9,10},{10,1... | collective-permute-start | bytes 835592 | tf_op jit(solution)/shard_map/ppermute | solution.py:22
  8.2 5.4 %collective-permute-start = (f32[17,8,256]{2,1,0:T(8,128)S(1)}, f32[17,8,256]{2,1,0:T(8,128)S(1)}, u32[]{:S(2)}, u32[]{:S(2)}) collective-permute-start(f32[17,8,256]{2,1,0:T(8,128)S(1)} %pad_maximum_fusion.3), channel_id=1, source_target_pairs={{0,4},{4,8},{8,12},{12,16},{16,20},{20,24},{24,28},{28,0},{1,5},{5... | collective-permute-start | bytes 417800 | tf_op jit(solution)/shard_map/ppermute | solution.py:22
  8.3 5.2 %collective-permute-start.1 = (f32[16,8,256]{2,1,0:T(8,128)S(1)}, f32[16,8,256]{2,1,0:T(8,128)S(1)}, u32[]{:S(2)}, u32[]{:S(2)}) collective-permute-start(f32[16,8,256]{2,1,0:T(8,128)S(1)} %pad_maximum_fusion.6), channel_id=1, source_target_pairs={{0,28},{4,0},{8,4},{12,8},{16,12},{20,16},{24,20},{28,24},{1,29},{... | collective-permute-start | bytes 393224 | tf_op jit(solution)/shard_map/ppermute | solution.py:22
  13.5 7.0 %copy-start.1 = (f32[16,8,256]{2,1,0:T(8,128)}, f32[16,8,256]{2,1,0:T(8,128)S(1)}, u32[]{:S(2)}) copy-start(f32[16,8,256]{2,1,0:T(8,128)S(1)} %collective-permute-done.1) | copy-start | bytes 393220
  13.7 6.9 %copy-start.2 = (f32[17,8,256]{2,1,0:T(8,128)}, f32[17,8,256]{2,1,0:T(8,128)S(1)}, u32[]{:S(2)}) copy-start(f32[17,8,256]{2,1,0:T(8,128)S(1)} %collective-permute-done) | copy-start | bytes 417796
  20.6 7.8 %slice-start = ((f32[16,8,256]{2,1,0:T(8,128)}), f32[4,8,256]{2,1,0:T(8,128)S(1)}, s32[]{:S(2)}) async-start(f32[16,8,256]{2,1,0:T(8,128)} %copy-done.1), calls=%async_computation.1 | async-start | bytes 65536 | tf_op jit(solution)/shard_map/slice | solution.py:315
  20.6 7.8 %slice-start.2 = ((f32[17,8,256]{2,1,0:T(8,128)}), f32[5,8,256]{2,1,0:T(8,128)S(1)}, s32[]{:S(2)}) async-start(f32[17,8,256]{2,1,0:T(8,128)} %copy-done.2), calls=%async_computation.3 | async-start | bytes 81920 | tf_op jit(solution)/shard_map/slice | solution.py:315
  20.7 5.1 %collective-permute-start.5 = (f32[17,8,256]{2,1,0:T(8,128)S(1)}, f32[17,8,256]{2,1,0:T(8,128)S(1)}, u32[]{:S(2)}, u32[]{:S(2)}) collective-permute-start(f32[17,8,256]{2,1,0:T(8,128)S(1)} %pad_maximum_fusion.4), channel_id=1, source_target_pairs={{0,28},{4,0},{8,4},{12,8},{16,12},{20,16},{24,20},{28,24},{1,29},{... | collective-permute-start | bytes 417800 | tf_op jit(solution)/shard_map/ppermute | solution.py:22
  21.8 7.4 %slice-start.1 = ((f32[16,8,256]{2,1,0:T(8,128)}), f32[12,8,256]{2,1,0:T(8,128)S(1)}, s32[]{:S(2)}) async-start(f32[16,8,256]{2,1,0:T(8,128)} %copy-done.1), calls=%async_computation.2 | async-start | bytes 196608 | tf_op jit(solution)/shard_map/slice | solution.py:311
  21.8 7.4 %slice-start.3 = ((f32[17,8,256]{2,1,0:T(8,128)}), f32[12,8,256]{2,1,0:T(8,128)S(1)}, s32[]{:S(2)}) async-start(f32[17,8,256]{2,1,0:T(8,128)} %copy-done.2), calls=%async_computation.4 | async-start | bytes 196608 | tf_op jit(solution)/shard_map/slice | solution.py:309
  21.8 6.0 %collective-permute-start.4 = (f32[18,8,256]{2,1,0:T(8,128)S(1)}, f32[18,8,256]{2,1,0:T(8,128)S(1)}, u32[]{:S(2)}, u32[]{:S(2)}) collective-permute-start(f32[18,8,256]{2,1,0:T(8,128)S(1)} %pad_maximum_fusion.2), channel_id=1, source_target_pairs={{0,4},{4,8},{8,12},{12,16},{16,20},{20,24},{24,28},{28,0},{1,5},{5... | collective-permute-start | bytes 442376 | tf_op jit(solution)/shard_map/ppermute | solution.py:22
